TPU v7x, 32 devices: a whole 2x2x4 slice. The times are simulated.
32 devices in a mesh: ctx: 16 (over z, x, core), tp: 2 (over y).
Axes of the slice: x: 2, y: 2, z: 4, core: 2. Of those that a mesh axis runs over, the one named last changes fastest.
Arguments:
- token_ids: int32 [12288], P('ctx'), may hold values from 0 to 511
- embed_table: bfloat16 [512, 4096], replicated, may hold values from -6 to 6
- norm_gain: float32 [4096], replicated, may hold values from 0.25 to 1.75
- w_in: bfloat16 [4096, 3, 2048], P(None, None, 'tp'), may hold values from -0.09375 to 0.09375
- short_taps: float32 [3, 3, 2048], P(None, None, 'tp'), may hold values from -3 to 3
- long_filter: bfloat16 [2048, 12288], P('tp', 'ctx'), may hold values from -0.0546875 to 0.0546875
- skip_gain: float32 [2048], P('tp'), may hold values from 0.5 to 2
- w_out: bfloat16 [2048, 4096], P(None, 'tp'), may hold values from -0.125 to 0.125
Outputs:
- mixed: bfloat16 [12288, 4096], P('ctx', 'tp')
All inputs are finite; a program needn't handle non-finite values.
Results may differ from a plain program's by a relative error of at most 0.0095.
Values may be sent and summed in bfloat16 or wider, within the bound.
A program may use at most 192 MiB of HBM per device.

v0:
```python
import math

import jax
import jax.numpy as jnp
from jax import lax
from jax.sharding import PartitionSpec as P

norm_eps = 1e-06


def shifted(block, axis, distance):
    devices = range(lax.axis_size(axis))
    route = [(i - distance, i) for i in devices if i - distance in devices]
    return lax.ppermute(block, axis, route)


def angle_table(outer, inner, period):
    product = (
        jnp.arange(outer, dtype=jnp.int32)[:, None]
        * jnp.arange(inner, dtype=jnp.int32)[None, :]
        % period
    )
    phase = product.astype(jnp.float32) * (2.0 * math.pi / period)
    return (jnp.cos(phase), jnp.sin(phase))


def contract(form, left, right):
    return jnp.einsum(
        form, left, right, precision=lax.Precision.HIGHEST, preferred_element_type=jnp.float32
    )


def forward_transform(signal, tables):
    cos_rows, sin_rows, cos_twist, sin_twist, cos_cols, sin_cols = tables
    first_real = contract("kn,cnm->ckm", cos_rows, signal)
    first_imag = -contract("kn,cnm->ckm", sin_rows, signal)
    turned_real = first_real * cos_twist + first_imag * sin_twist
    turned_imag = first_imag * cos_twist - first_real * sin_twist
    spec_real = contract("ckm,mj->ckj", turned_real, cos_cols) + contract(
        "ckm,mj->ckj", turned_imag, sin_cols
    )
    spec_imag = contract("ckm,mj->ckj", turned_imag, cos_cols) - contract(
        "ckm,mj->ckj", turned_real, sin_cols
    )
    return (spec_real, spec_imag)


def inverse_transform(spec_real, spec_imag, tables, period):
    cos_rows, sin_rows, cos_twist, sin_twist, cos_cols, sin_cols = tables
    back_real = contract("ckj,mj->ckm", spec_real, cos_cols) - contract(
        "ckj,mj->ckm", spec_imag, sin_cols
    )
    back_imag = contract("ckj,mj->ckm", spec_imag, cos_cols) + contract(
        "ckj,mj->ckm", spec_real, sin_cols
    )
    untwist_real = back_real * cos_twist - back_imag * sin_twist
    untwist_imag = back_imag * cos_twist + back_real * sin_twist
    signal = contract("kn,ckm->cnm", cos_rows, untwist_real) - contract(
        "kn,ckm->cnm", sin_rows, untwist_imag
    )
    return signal / period


def causal_conv(signal, kernel):
    channels = signal.shape[0]
    length = signal.shape[1]
    col_count = min(256, length)
    row_count = 2 * length // col_count
    half_rows = length // col_count
    cos_rows, sin_rows = angle_table(row_count, half_rows, row_count)
    cos_twist, sin_twist = angle_table(row_count, col_count, row_count * col_count)
    cos_cols, sin_cols = angle_table(col_count, col_count, col_count)
    tables = (cos_rows, sin_rows, cos_twist, sin_twist, cos_cols, sin_cols)
    signal_real, signal_imag = forward_transform(
        signal.astype(jnp.float32).reshape(channels, half_rows, col_count), tables
    )
    kernel_real, kernel_imag = forward_transform(
        kernel.astype(jnp.float32).reshape(channels, half_rows, col_count), tables
    )
    joint_real = signal_real * kernel_real - signal_imag * kernel_imag
    joint_imag = signal_real * kernel_imag + signal_imag * kernel_real
    result = inverse_transform(joint_real, joint_imag, tables, row_count * col_count)
    return result.reshape(channels, length)


def local(token_ids, embed_table, norm_gain, w_in, short_taps, long_filter, skip_gain, w_out):
    vocab = embed_table.shape[0]
    one_hot = (token_ids[:, None] == jnp.arange(vocab, dtype=jnp.int32)[None, :]).astype(
        jnp.bfloat16
    )
    embedded = jnp.dot(one_hot, embed_table, preferred_element_type=jnp.float32)
    scale = lax.rsqrt(jnp.mean(embedded * embedded, axis=1, keepdims=True) + norm_eps)
    normed = (embedded * scale * norm_gain).astype(jnp.bfloat16)
    width = w_in.shape[0]
    chan_part = w_in.shape[2]
    flat_proj = jnp.dot(
        normed, w_in.reshape(width, 3 * chan_part), preferred_element_type=jnp.float32
    ).astype(jnp.bfloat16)
    projected = jnp.transpose(flat_proj.reshape(-1, 3, chan_part), (1, 2, 0))
    positions = projected.shape[2]
    edge = projected[:, :, positions - 2 :]
    prior = shifted(edge, "ctx", 1)
    extended = jnp.concatenate([prior, projected], axis=2).astype(jnp.float32)
    shortened = (
        short_taps[0][:, :, None] * extended[:, :, 2:]
        + short_taps[1][:, :, None] * extended[:, :, 1 : positions + 1]
        + short_taps[2][:, :, None] * extended[:, :, 0:positions]
    ).astype(jnp.bfloat16)
    query_side = shortened[0]
    key_side = shortened[1]
    value_side = shortened[2]
    local_channels = shortened.shape[1]
    groups = lax.axis_size("ctx")
    owned = local_channels // groups

    def spread(array):
        return array.reshape(groups, owned, array.shape[-1])

    first_channel = lax.axis_index("ctx") * owned
    own_skip = lax.dynamic_slice_in_dim(skip_gain, first_channel, owned)[:, None]
    product_local = (key_side.astype(jnp.float32) * value_side.astype(jnp.float32)).astype(
        jnp.bfloat16
    )
    arrived = (
        lax.all_to_all(spread(product_local), "ctx", split_axis=0, concat_axis=2, tiled=True),
        lax.all_to_all(spread(long_filter), "ctx", split_axis=0, concat_axis=2, tiled=True),
    )
    product = arrived[0].reshape(owned, -1)
    filter_full = arrived[1].reshape(owned, -1)
    convolved = causal_conv(product, filter_full)
    outgoing = (convolved + own_skip * product.astype(jnp.float32)).astype(jnp.bfloat16)
    returned = lax.all_to_all(
        outgoing.reshape(1, owned, -1), "ctx", split_axis=2, concat_axis=0, tiled=True
    )
    returned = returned.reshape(local_channels, positions)
    gated = (query_side.astype(jnp.float32) * returned.astype(jnp.float32)).astype(jnp.bfloat16)
    width_part = w_out.shape[1]
    projected_out = jnp.dot(
        lax.all_gather(gated, "tp", axis=0, tiled=True).T, w_out, preferred_element_type=jnp.float32
    )
    residual = lax.dynamic_slice_in_dim(embedded, lax.axis_index("tp") * width_part, width_part, 1)
    return (residual + projected_out).astype(jnp.bfloat16)


def solution(mesh):
    return jax.shard_map(
        local,
        mesh=mesh,
        in_specs=(
            P("ctx"),
            P(),
            P(),
            P(None, None, "tp"),
            P(None, None, "tp"),
            P("tp", "ctx"),
            P("tp"),
            P(None, "tp"),
        ),
        out_specs=P("ctx", "tp"),
        check_vma=False,
    )
```

profile of v0, /device:TPU:0, one launch (start us, length us, event | category | flops | bytes accessed | tf_op | source)
XLA Modules:
  0.0 508.4 jit_solution(8029366977371177981)
XLA Ops:
  6.5 7.4 %all-to-all-start.1 = ((bf16[16,64,768]{2,1,0:T(8,128)(2,1)}), bf16[16,64,768]{2,1,0:T(8,128)(2,1)S(1)}, u32[]{:S(2)}, u32[]{:S(2)}) async-start(bf16[16,64,768]{2,1,0:T(8,128)(2,1)} %bitcast.149), calls=%async_computation.1 | async-start | bytes 3145728 | tf_op jit(solution)/shard_map/all_to_all | solution.py:126
  13.9 8.8 %multiply_reduce_fusion = (f32[768]{0:T(1024)S(1)}, f32[768,4096]{1,0:T(8,128)}) fusion(bf16[512,4096]{1,0:T(8,128)(2,1)} %param.9, s32[768]{0:T(1024)} %param.8), kind=kOutput, calls=%fused_computation.1 | convolution fusion | flops 3227909376 | bytes 16783360 | tf_op jit(solution)/shard_map/dot_general | solution.py:91
  22.7 33.5 %copy.32 = bf16[4096,3,1024]{0,2,1:T(8,128)(2,1)} copy(bf16[4096,3,1024]{2,0,1:T(8,128)(2,1)} %param.11) | data formatting | bytes 50331648 | tf_op args[3]
  56.2 27.9 %fusion.24 = bf16[768,3072]{1,0:T(8,128)(2,1)} fusion(bf16[4096,3072]{0,1:T(8,128)(2,1)} %bitcast.138, f32[768,4096]{1,0:T(8,128)} %get-tuple-element.11, f32[4096]{0:T(1024)S(1)} %copy-done.9, f32[768]{0:T(1024)S(1)} %add_rsqrt_fusion), kind=kOutput, calls=%fused_computation.39 | convolution fusion | flops 19339149312 | bytes 42486784 | tf_op jit(solution)/shard_map/dot_general | solution.py:96
  84.1 6.6 %copy.33 = bf16[768,3072]{0,1:T(8,128)(2,1)} copy(bf16[768,3072]{1,0:T(8,128)(2,1)} %fusion.24) | data formatting | bytes 9437184 | tf_op jit(solution)/shard_map/convert_element_type | solution.py:98
  90.8 1.4 slice.40
  92.2 0.3 copy.34
  92.5 2.5 collective-permute-start
  95.0 0.4 fusion.86
  95.4 0.8 dynamic_slice.7
  96.2 0.0 collective-permute-done
  96.2 0.4 copy.35
  96.6 4.8 maximum_convert_fusion
  101.4 8.1 %fusion.1 = bf16[3,1024,768]{2,1,0:T(8,128)(2,1)S(1)} fusion(f32[3,1024,770]{2,1,0:T(8,128)S(1)} %maximum_convert_fusion, f32[3,1024]{1,0:T(4,128)S(1)} %get-tuple-element.8, f32[3,1024]{1,0:T(4,128)S(1)} %get-tuple-element.9, f32[3,1024]{1,0:T(4,128)S(1)} %get-tuple-element.7), kind=kLoop, calls=%fused_computation.4 | loop fusion | flops 14155776 | bytes 33067008 | tf_op jit(solution)/shard_map/convert_element_type | solution.py:108
  109.5 2.2 copy-done.3
  111.7 1.5 multiply_convert_fusion.4
  113.3 0.0 all-to-all-done.1
  113.3 1.1 copy-done.7
  114.4 7.3 %all-to-all-start = ((bf16[16,64,768]{2,1,0:T(8,128)(2,1)}), bf16[16,64,768]{2,1,0:T(8,128)(2,1)S(1)}, u32[]{:S(2)}, u32[]{:S(2)}) async-start(bf16[16,64,768]{2,1,0:T(8,128)(2,1)} %bitcast.147), calls=%async_computation | async-start | bytes 3145728 | tf_op jit(solution)/shard_map/all_to_all | solution.py:125
  121.8 0.3 all-gather.2.cloned.1.call-start
  122.0 3.5 copy.37
  125.5 3.7 reshape.134
  129.2 4.3 fusion.92
  133.6 2.8 fusion.97
  136.3 9.2 %fusion.10 = f32[64,96,256]{2,1,0:T(8,128)} fusion(f32[96,64,256]{2,0,1:T(8,128)S(1)} %fusion.97, f32[96,64,256]{2,0,1:T(8,128)S(1)} %fusion.92, f32[96,256]{1,0:T(8,128)S(1)} %get-tuple-element.12, f32[96,256]{1,0:T(8,128)S(1)} %get-tuple-element.13), kind=kOutput, calls=%fused_computation.15 | convolution fusion | flops 4839047168 | bytes 19070976 | tf_op jit(solution)/shard_map/ckm,mj->ckj/dot_general | solution.py:28
  145.6 9.4 %fusion.6 = f32[64,96,256]{2,1,0:T(8,128)} fusion(f32[96,64,256]{2,0,1:T(8,128)S(1)} %fusion.97, f32[96,64,256]{2,0,1:T(8,128)S(1)} %fusion.92, f32[96,256]{1,0:T(8,128)S(1)} %get-tuple-element.12, f32[96,256]{1,0:T(8,128)S(1)} %get-tuple-element.13), kind=kOutput, calls=%fused_computation.11 | convolution fusion | flops 4839047168 | bytes 19070976 | tf_op jit(solution)/shard_map/ckm,mj->ckj/dot_general | solution.py:28
  155.0 9.1 %fusion.8 = f32[64,96,256]{2,1,0:T(8,128)} fusion(f32[96,64,256]{2,0,1:T(8,128)S(1)} %fusion.97, f32[96,64,256]{2,0,1:T(8,128)S(1)} %fusion.92, f32[96,256]{1,0:T(8,128)S(1)} %get-tuple-element.12, f32[96,256]{1,0:T(8,128)S(1)} %get-tuple-element.13), kind=kOutput, calls=%fused_computation.13 | convolution fusion | flops 4839047168 | bytes 19070976 | tf_op jit(solution)/shard_map/ckm,mj->ckj/dot_general | solution.py:28
  164.1 0.0 all-to-all-done
  164.1 2.0 copy.36
  166.1 4.2 reshape.132
  170.3 4.4 fusion.94
  174.8 2.7 fusion.99
  177.5 9.2 %fusion.37 = f32[64,96,256]{2,1,0:T(8,128)} fusion(f32[64,256,96]{1,2,0:T(8,128)S(1)} %fusion.99, f32[64,256,96]{1,2,0:T(8,128)S(1)} %fusion.94, f32[96,256]{1,0:T(8,128)S(1)} %get-tuple-element.12, f32[96,256]{1,0:T(8,128)S(1)} %get-tuple-element.13), kind=kOutput, calls=%fused_computation.59 | convolution fusion | flops 4839047168 | bytes 19070976 | tf_op jit(solution)/shard_map/ckm,mj->ckj/dot_general | solution.py:28
  186.7 9.3 %fusion.41 = f32[64,96,256]{2,1,0:T(8,128)} fusion(f32[64,256,96]{1,2,0:T(8,128)S(1)} %fusion.99, f32[64,256,96]{1,2,0:T(8,128)S(1)} %fusion.94, f32[96,256]{1,0:T(8,128)S(1)} %get-tuple-element.12, f32[96,256]{1,0:T(8,128)S(1)} %get-tuple-element.13), kind=kOutput, calls=%fused_computation.61 | convolution fusion | flops 4839047168 | bytes 19070976 | tf_op jit(solution)/shard_map/ckm,mj->ckj/dot_general | solution.py:28
  196.0 9.3 %fusion.39 = f32[64,96,256]{2,1,0:T(8,128)} fusion(f32[64,256,96]{1,2,0:T(8,128)S(1)} %fusion.99, f32[64,256,96]{1,2,0:T(8,128)S(1)} %fusion.94, f32[96,256]{1,0:T(8,128)S(1)} %get-tuple-element.12, f32[96,256]{1,0:T(8,128)S(1)} %get-tuple-element.13), kind=kOutput, calls=%fused_computation.60 | convolution fusion | flops 4839047168 | bytes 19070976 | tf_op jit(solution)/shard_map/ckm,mj->ckj/dot_general | solution.py:28
  205.3 9.2 %fusion.35 = f32[64,96,256]{2,1,0:T(8,128)} fusion(f32[64,256,96]{1,2,0:T(8,128)S(1)} %fusion.99, f32[64,256,96]{1,2,0:T(8,128)S(1)} %fusion.94, f32[96,256]{1,0:T(8,128)S(1)} %get-tuple-element.12, f32[96,256]{1,0:T(8,128)S(1)} %get-tuple-element.13), kind=kOutput, calls=%fused_computation.58 | convolution fusion | flops 4839047168 | bytes 19070976 | tf_op jit(solution)/shard_map/ckm,mj->ckj/dot_general | solution.py:28
  214.5 24.4 %multiply_subtract_fusion = (f32[64,96,256]{2,1,0:T(8,128)}, f32[64,96,256]{2,1,0:T(8,128)}) fusion(f32[64,96,256]{2,1,0:T(8,128)} %fusion.8, f32[64,96,256]{2,1,0:T(8,128)} %fusion.35, f32[64,96,256]{2,1,0:T(8,128)} %fusion.39, f32[64,96,256]{2,1,0:T(8,128)} %fusion.10, f32[64,96,256]{2,1,0:T(8,128)} %fusion.6, f32[64,96,256]{2,1,0:T(8,128)} %fusion.41, ...), kind=kOutput, calls=%fused_computation.33 | convolution fusion | flops 4854775808 | bytes 69402624 | tf_op jit(solution)/shard_map/ckm,mj->ckj/dot_general | solution.py:28
  238.9 0.0 slice-start.2
  238.9 10.0 %fusion.51 = f32[64,96,256]{2,1,0:T(8,128)S(1)} fusion(f32[64,96,256]{2,1,0:T(8,128)} %get-tuple-element.6), kind=kOutput, calls=%fused_computation.71 | convolution fusion | flops 4832755712 | bytes 12582912 | tf_op jit(solution)/shard_map/ckj,mj->ckm/dot_general | solution.py:28
  248.9 0.0 slice-start.3
  248.9 6.3 %fusion.57 = f32[64,96,256]{2,1,0:T(8,128)S(1)} fusion(f32[64,96,256]{2,1,0:T(8,128)S(1)} %copy-done.2), kind=kOutput, calls=%fused_computation.77 | convolution fusion | flops 4832755712 | bytes 12582912 | tf_op jit(solution)/shard_map/ckj,mj->ckm/dot_general | solution.py:28
  255.2 6.4 %fusion.49 = f32[64,96,256]{2,1,0:T(8,128)S(1)} fusion(f32[64,96,256]{2,1,0:T(8,128)S(1)} %bitcast.137), kind=kOutput, calls=%fused_computation.69 | convolution fusion | flops 4832755712 | bytes 12582912 | tf_op jit(solution)/shard_map/ckj,mj->ckm/dot_general | solution.py:28
  261.7 8.9 %fusion.59 = f32[64,96,256]{2,1,0:T(8,128)} fusion(f32[64,96,256]{2,1,0:T(8,128)S(1)} %bitcast.137), kind=kOutput, calls=%fused_computation.79 | convolution fusion | flops 4832755712 | bytes 12582912 | tf_op jit(solution)/shard_map/ckj,mj->ckm/dot_general | solution.py:28
  270.6 8.3 %fusion.14 = f32[64,256,48]{1,2,0:T(8,128)} fusion(f32[96,256]{1,0:T(8,128)S(1)} %get-tuple-element.12, f32[96,256]{1,0:T(8,128)S(1)} %get-tuple-element.13, f32[64,96,256]{2,1,0:T(8,128)S(1)} %fusion.57, f32[64,96,256]{2,1,0:T(8,128)S(1)} %fusion.49, f32[64,96,256]{2,1,0:T(8,128)} %fusion.59, f32[64,96,256]{2,1,0:T(8,128)S(1)} %fusion.51), kind=kOutput, calls=%fused_computation.24 | convolution fusion | flops 913875456 | bytes 28508160 | tf_op jit(solution)/shard_map/kn,ckm->cnm/dot_general | solution.py:28
  278.9 8.9 %multiply_bitcast_fusion = f32[64,48,256]{2,1,0:T(8,128)} fusion(f32[64,256,48]{1,2,0:T(8,128)} %fusion.14, f32[96,256]{1,0:T(8,128)S(1)} %get-tuple-element.12, f32[96,256]{1,0:T(8,128)S(1)} %get-tuple-element.13, f32[64,96,256]{2,1,0:T(8,128)S(1)} %fusion.57, f32[64,96,256]{2,1,0:T(8,128)S(1)} %fusion.49, f32[64,96,256]{2,1,0:T(8,128)} %fusion.59, ...), kind=kOutput, calls=%fused_computation.45 | convolution fusion | flops 915448320 | bytes 31653888 | tf_op jit(solution)/shard_map/kn,ckm->cnm/dot_general | solution.py:28
  287.8 4.3 reshape.135
  292.1 0.3 convert_bitcast_fusion
  292.4 0.3 copy.42
  292.7 1.2 copy-done.6
  294.0 0.3 add_convert_fusion.1
  294.3 10.0 %copy.39 = bf16[1,64,12288]{1,0,2:T(2,128)(2,1)} copy(bf16[1,64,12288]{2,1,0:T(8,128)(2,1)S(1)} %add_convert_fusion.1) | data formatting | bytes 3145728 | tf_op jit(solution)/shard_map/convert_element_type | solution.py:131
  304.3 0.5 broadcast.134
  304.8 67.2 %reduce = bf16[12288,64]{1,0:T(8,128)(2,1)S(1)} reduce(bf16[12288,1,64]{2,1,0:T(2,128)(2,1)} %bitcast.139, bf16[]{:T(256)} %broadcast.134), dimensions={1}, to_apply=%bitcast.115.reduce_sub_computation | reduce | bytes 3145730
  372.0 3.2 reshape.144
  375.2 42.2 %all_to_all.39 = bf16[16,2,24576]{2,1,0:T(2,128)(2,1)S(1)} all-to-all(bf16[16,2,24576]{2,1,0:T(2,128)(2,1)} %reshape.144), channel_id=1, replica_groups=mesh['ctx'=16,'tp'=2] {'ctx'}, dimensions={0} | all-to-all | bytes 3145728 | tf_op jit(solution)/shard_map/all_to_all | solution.py:132
  417.4 7.8 %reshape.145 = bf16[12288,1,64]{2,1,0:T(2,128)(2,1)} reshape(bf16[16,2,24576]{2,1,0:T(2,128)(2,1)S(1)} %all_to_all.39) | data formatting | bytes 3145728
  425.2 11.9 %copy.40 = bf16[1,64,12288]{2,1,0:T(8,128)(2,1)S(1)} copy(bf16[1,64,12288]{1,0,2:T(2,128)(2,1)} %bitcast.140) | data formatting | bytes 3145728 | tf_op jit(solution)/shard_map/all_to_all | solution.py:132
  437.1 0.4 copy.43
  437.6 0.2 bitcast_bitcast_fusion
  437.8 1.8 copy.41
  439.6 3.2 fusion.25
  442.8 0.0 all-gather.2.cloned.1.call-update
  442.9 45.5 %all-gather.2.cloned.1.call-done = bf16[2048,768]{1,0:T(8,128)(2,1)} async-done(((bf16[1024,768]{1,0:T(8,128)(2,1)}), bf16[2048,768]{1,0:T(8,128)(2,1)}) %all-gather.2.cloned.1.call-update) | async-done | bytes 3145744 | tf_op jit(solution)/shard_map/all_gather | solution.py:139
  488.4 13.0 %add_convert_fusion = bf16[768,2048]{1,0:T(8,128)(2,1)} fusion(f32[768,4096]{1,0:T(8,128)} %get-tuple-element.11, s32[]{:T(128)S(6)} %select_n.86, bf16[2048,768]{1,0:T(8,128)(2,1)} %all-gather.2.cloned.1.call-done, bf16[2048,2048]{1,0:T(8,128)(2,1)} %param.15), kind=kOutput, calls=%fused_computation.23 | convolution fusion | flops 6445596672 | bytes 20971524 | tf_op jit(solution)/shard_map/dot_general | solution.py:138
  (27 shorter events, 0.1 us)
Async XLA Ops:
  6.5 106.7 %all-to-all-start.1 = ((bf16[16,64,768]{2,1,0:T(8,128)(2,1)}), bf16[16,64,768]{2,1,0:T(8,128)(2,1)S(1)}, u32[]{:S(2)}, u32[]{:S(2)}) async-start(bf16[16,64,768]{2,1,0:T(8,128)(2,1)} %bitcast.149), calls=%async_computation.1 | async-start | bytes 3145728 | tf_op jit(solution)/shard_map/all_to_all | solution.py:126
  22.7 33.5 %copy-start.9 = (f32[4096]{0:T(1024)S(1)}, f32[4096]{0:T(1024)}, u32[]{:S(2)}) copy-start(f32[4096]{0:T(1024)} %param.10) | copy-start | bytes 49156
  84.1 10.8 %copy-start.8 = (f32[3,3,1024]{2,1,0:T(4,128)S(1)}, f32[3,3,1024]{2,1,0:T(4,128)}, u32[]{:S(2)}) copy-start(f32[3,3,1024]{2,1,0:T(4,128)} %param.12) | copy-start | bytes 110596
  92.5 3.7 collective-permute-start
  109.5 2.2 copy-start.3
  113.3 1.1 copy-start.7
  114.4 49.7 %all-to-all-start = ((bf16[16,64,768]{2,1,0:T(8,128)(2,1)}), bf16[16,64,768]{2,1,0:T(8,128)(2,1)S(1)}, u32[]{:S(2)}, u32[]{:S(2)}) async-start(bf16[16,64,768]{2,1,0:T(8,128)(2,1)} %bitcast.147), calls=%async_computation | async-start | bytes 3145728 | tf_op jit(solution)/shard_map/all_to_all | solution.py:125
  121.8 366.6 %all-gather.2.cloned.1.call-start = ((), (), s32[]{:S(2)}) async-start(), calls=%async_computation.3 | async-start | bytes 4718592 | tf_op jit(solution)/shard_map/all_gather | solution.py:139
  129.2 4.3 copy-start.4
  133.5 21.4 %copy-start = (f32[96,64,256]{2,0,1:T(8,128)}, f32[96,64,256]{2,0,1:T(8,128)S(1)}, u32[]{:S(2)}) copy-start(f32[96,64,256]{2,0,1:T(8,128)S(1)} %fusion.92) | copy-start | bytes 18874372
  136.3 18.7 %copy-start.1 = (f32[96,64,256]{2,0,1:T(8,128)}, f32[96,64,256]{2,0,1:T(8,128)S(1)}, u32[]{:S(2)}) copy-start(f32[96,64,256]{2,0,1:T(8,128)S(1)} %fusion.97) | copy-start | bytes 18874372
  170.3 4.4 copy-start.5
  196.0 18.4 %slice-start = ((s8[6291456]{0:T(1024)(128)(4,1)}), s8[4194304]{0:T(1024)(128)(4,1)S(1)}, s32[]{:S(2)}) async-start(s8[6291456]{0:T(1024)(128)(4,1)} %bitcast.134), calls=%async_computation.4 | async-start | bytes 8388608
  205.3 9.2 %slice-start.1 = ((s8[6291456]{0:T(1024)(128)(4,1)}), s8[2097152]{0:T(1024)(128)(4,1)S(1)}, s32[]{:S(2)}) async-start(s8[6291456]{0:T(1024)(128)(4,1)} %bitcast.134), calls=%async_computation.5 | async-start | bytes 4194304
  238.9 10.0 %copy-start.2 = (f32[64,96,256]{2,1,0:T(8,128)S(1)}, f32[64,96,256]{2,1,0:T(8,128)}, u32[]{:S(2)}) copy-start(f32[64,96,256]{2,1,0:T(8,128)} %get-tuple-element.6) | copy-start | bytes 18874372
  238.9 16.3 %slice-start.2 = ((s8[6291456]{0:T(1024)(128)(4,1)}), s8[4194304]{0:T(1024)(128)(4,1)S(1)}, s32[]{:S(2)}) async-start(s8[6291456]{0:T(1024)(128)(4,1)} %bitcast.136), calls=%async_computation.6 | async-start | bytes 8388608
  248.9 6.3 %slice-start.3 = ((s8[6291456]{0:T(1024)(128)(4,1)}), s8[2097152]{0:T(1024)(128)(4,1)S(1)}, s32[]{:S(2)}) async-start(s8[6291456]{0:T(1024)(128)(4,1)} %bitcast.136), calls=%async_computation.7 | async-start | bytes 4194304
  292.1 1.9 copy-start.6
Sparse Core Ops, SparseCore 0:
  443.0 45.3 all-gather.1
where the time goes:
time: 516 us; the launch traced here: 508 us
  matrix products  202 us (39%)
  local copies, waits for them, and re-layouts  102 us (20%)
  other arithmetic  85.9 us (17%)
  waiting for transfers between devices  45.5 us (9%)
  blocking collectives  42.2 us (8%)
  starting transfers between devices  17.4 us (3%)
  between operations  14 us (3%)
    dot_general x18, matrix products, contract(): jnp.einsum(form, left, right, precision=lax.Precision.HIGHEST, preferred_...  152 us
    unnamed x4, other arithmetic  67.5 us
    unnamed x33, local copies, waits for them, and re-layouts  50.2 us
    all_gather x1, waiting for transfers between devices, local(): lax.all_gather(gated, 'tp', axis=0, tiled=True)  45.5 us
    all_to_all x1, blocking collectives, local(): lax.all_to_all(outgoing.reshape(1, owned, -1), 'ctx', split_axis=2, conca...  42.2 us
    dot_general x1, matrix products, local(): jnp.dot(normed, w_in.reshape(width, 3 * chan_part), preferred_element_typ...  27.9 us
    dot_general x1, matrix products, local(): jnp.dot(lax.all_gather(gated, 'tp', axis=0, tiled=True).T, w_out, preferr...  13 us
    all_to_all x1, local copies, waits for them, and re-layouts, local(): lax.all_to_all(outgoing.reshape(1, owned, -1), 'ctx', split_axis=2, conca...  11.9 us
  transfers between devices with their start and end apart: 4, of which 1 were waited for; matrix products, arithmetic and copies ran while one was open for 27% of the time, Pallas kernels for 0%

commit v1 on v0

v1 whole, which is shorter than its diff:
```python
import functools
import math

import jax
import jax.numpy as jnp
import numpy as np
from jax import lax
from jax.experimental import pallas as pl
from jax.experimental.pallas import tpu as pltpu
from jax.sharding import PartitionSpec as P

norm_eps = 1e-06
lanes = 128
wide = 256


def transform_tables(length):
    period = 2 * length
    rows = length // lanes
    kept = rows + 1
    padded = -(-kept // 16) * 16
    coarse = np.zeros((2 * padded, rows))
    grid = 2 * np.pi * (np.outer(np.arange(kept), np.arange(rows)) % (2 * rows)) / (2 * rows)
    coarse[:kept] = np.cos(grid)
    coarse[padded : padded + kept] = -np.sin(grid)
    weight = np.full((kept, 1), 2.0)
    weight[0] = weight[-1] = 1.0
    back = np.zeros((rows, 2 * padded))
    back[:, :kept] = (weight * np.cos(grid)).T / period
    back[:, padded : padded + kept] = -(weight * np.sin(grid)).T / period
    turn = 2 * np.pi * np.outer(np.arange(padded), np.arange(lanes)) / period
    fine = 2 * np.pi * (np.outer(np.arange(lanes), np.arange(lanes)) % lanes) / lanes
    cos, sin = np.cos(fine), np.sin(fine)
    forward = np.block([[cos, -sin], [sin, cos]])
    inverse = np.block([[cos, sin], [-sin, cos]])
    half = jnp.bfloat16
    return (
        coarse.astype(half),
        np.cos(turn).astype(np.float32),
        np.sin(turn).astype(np.float32),
        forward.astype(half),
        inverse.astype(half),
        back.astype(half),
    )


def mul(left, right):
    return jnp.dot(left, right, preferred_element_type=jnp.float32)


def block_kernel(
    tok_ref, tab_ref, taps_ref, skip_ref, h_ref,
    coarse_ref, cos_ref, sin_ref, fwd_ref, inv_ref, back_ref,
    out_ref, pf, hf, q_s, p_s, *, stride, unroll,
):
    half = jnp.bfloat16
    full = jnp.float32
    sources, chans, span = h_ref.shape
    per = span // lanes
    blocks = sources * per
    vocab = tab_ref.shape[1]
    rows3 = 3 * chans
    padded = cos_ref.shape[0]

    words = lax.broadcasted_iota(jnp.int32, (vocab, wide), 0)
    lane = lax.broadcasted_iota(jnp.int32, (rows3, lanes), 1)

    def project(step, carry):
        one_back, two_back = carry
        picked = jnp.where(words == tok_ref[pl.ds(step, 1), :], 1.0, 0.0).astype(half)
        both = mul(tab_ref[...], picked).astype(half).astype(full)
        for part in range(wide // lanes):
            now = both[:, part * lanes : (part + 1) * lanes]
            once = pltpu.roll(now, 1, 1)
            twice = pltpu.roll(now, 2, 1)
            short = (
                taps_ref[0] * now
                + taps_ref[1] * jnp.where(lane < 1, one_back, once)
                + taps_ref[2] * jnp.where(lane < 2, two_back, twice)
            ).astype(half)
            one_back, two_back = once, twice
            key = short[chans : 2 * chans].astype(full)
            value = short[2 * chans :].astype(full)
            product = (key * value).astype(half)
            at = step * (wide // lanes) + part
            q_s[at] = short[:chans]
            p_s[at] = product
            pf[pl.ds(at, chans, stride=stride), :] = product.astype(full)
        return one_back, two_back

    zero = jnp.zeros((rows3, lanes), full)
    lax.fori_loop(0, blocks * lanes // wide, project, (zero, zero))

    def take(source, _):
        for part in range(per):
            tile = h_ref[source, :, part * lanes : (part + 1) * lanes]
            hf[pl.ds(source * per + part, chans, stride=stride), :] = tile.astype(full)
        return 0

    lax.fori_loop(0, sources, take, 0)

    def convolve(step, _):
        for sub in range(unroll):
            first = pl.multiple_of((step * unroll + sub) * stride, 8)
            here = pl.ds(first, blocks)
            pair = jnp.concatenate([pf[here, :].astype(half), hf[here, :].astype(half)], axis=1)
            staged = mul(coarse_ref[...], pair)
            cos, sin = cos_ref[...], sin_ref[...]

            def turned(lo):
                real = staged[:padded, lo : lo + lanes]
                imag = staged[padded:, lo : lo + lanes]
                return jnp.concatenate(
                    [(real * cos + imag * sin).astype(half), (imag * cos - real * sin).astype(half)],
                    axis=1,
                )

            spectra = mul(jnp.concatenate([turned(0), turned(lanes)], axis=0), fwd_ref[...])
            pr, pi = spectra[:padded, :lanes], spectra[:padded, lanes:]
            hr, hi = spectra[padded:, :lanes], spectra[padded:, lanes:]
            joint = jnp.concatenate(
                [(pr * hr - pi * hi).astype(half), (pr * hi + pi * hr).astype(half)], axis=1
            )
            undone = mul(joint, inv_ref[...])
            br, bi = undone[:, :lanes], undone[:, lanes:]
            stacked = jnp.concatenate(
                [(br * cos - bi * sin).astype(half), (bi * cos + br * sin).astype(half)], axis=0
            )
            pf[here, :] = mul(back_ref[...], stacked)
        return 0

    lax.fori_loop(0, chans // unroll, convolve, 0)

    def finish(source, _):
        for part in range(per):
            at = source * per + part
            convolved = pf[pl.ds(at, chans, stride=stride), :]
            skipped = (convolved + skip_ref[...] * p_s[at].astype(full)).astype(half)
            gated = q_s[at].astype(full) * skipped.astype(full)
            out_ref[source, :, part * lanes : (part + 1) * lanes] = gated.astype(half)
        return 0

    lax.fori_loop(0, sources, finish, 0)


def long_block(tokens, table, taps, skip, filters, chans):
    groups, _, span = filters.shape
    length = groups * span
    blocks = length // lanes
    stride = blocks + 8
    tables = transform_tables(length)
    unroll = math.gcd(chans, 4)
    vmem = pl.BlockSpec(memory_space=pltpu.VMEM)
    return pl.pallas_call(
        functools.partial(block_kernel, stride=stride, unroll=unroll),
        out_shape=jax.ShapeDtypeStruct((groups, chans, span), jnp.bfloat16),
        in_specs=[vmem] * 11,
        out_specs=vmem,
        scratch_shapes=[
            pltpu.VMEM((chans * stride, lanes), jnp.float32),
            pltpu.VMEM((chans * stride, lanes), jnp.float32),
            pltpu.VMEM((blocks, chans, lanes), jnp.bfloat16),
            pltpu.VMEM((blocks, chans, lanes), jnp.bfloat16),
        ],
        compiler_params=pltpu.CompilerParams(vmem_limit_bytes=48 * 1024 * 1024),
        cost_estimate=pl.CostEstimate(
            flops=40_000_000_000, bytes_accessed=8_000_000, transcendentals=0
        ),
    )(tokens.reshape(length // wide, wide), table, taps, skip, filters, *map(jnp.asarray, tables))


def local(token_ids, embed_table, norm_gain, w_in, short_taps, long_filter, skip_gain, w_out):
    half = jnp.bfloat16
    vocab, width = embed_table.shape
    local_channels = w_in.shape[2]
    groups = lax.axis_size("ctx")
    parts = lax.axis_size("tp")
    me = lax.axis_index("tp")
    chans = local_channels // groups
    first = lax.axis_index("ctx") * chans
    span = token_ids.shape[0]

    filters = lax.all_to_all(
        long_filter.reshape(groups, chans, span), "ctx", split_axis=0, concat_axis=0, tiled=True
    )
    tokens = lax.all_gather(token_ids, "ctx", axis=0, tiled=True)

    rows = embed_table.astype(jnp.float32)
    scale = lax.rsqrt(jnp.mean(rows * rows, axis=1, keepdims=True) + norm_eps)
    normed = (rows * scale * norm_gain).astype(half)
    own_w = lax.dynamic_slice_in_dim(w_in, first, chans, 2).reshape(width, 3 * chans)
    table = lax.dot_general(
        own_w, normed, (((0,), (1,)), ((), ())), preferred_element_type=jnp.float32
    ).astype(half)
    taps = lax.dynamic_slice_in_dim(short_taps, first, chans, 2).reshape(-1, 3 * chans, 1)
    skip = lax.dynamic_slice_in_dim(skip_gain, first, chans)[:, None]

    gated = long_block(tokens, table, taps, skip, filters, chans)
    mine = lax.all_to_all(gated, "ctx", split_axis=0, concat_axis=0, tiled=True)
    mine = mine.reshape(local_channels, span)

    columns = w_out.shape[1]
    one_hot = (token_ids[:, None] == jnp.arange(vocab, dtype=jnp.int32)[None, :]).astype(half)
    own_embed = lax.dynamic_slice_in_dim(embed_table, me * columns, columns, 1)
    total = jnp.dot(one_hot, own_embed, preferred_element_type=jnp.float32)
    for step in range(parts):
        if step == 0:
            piece = mine
        else:
            route = [(i, (i + step) % parts) for i in range(parts)]
            piece = lax.ppermute(mine, "tp", route)
        owner = lax.rem(me - step + parts, parts)
        own_rows = lax.dynamic_slice_in_dim(w_out, owner * local_channels, local_channels, 0)
        total = total + lax.dot_general(
            piece, own_rows, (((0,), (0,)), ((), ())), preferred_element_type=jnp.float32
        )
    return total.astype(half)


def solution(mesh):
    return jax.shard_map(
        local,
        mesh=mesh,
        in_specs=(
            P("ctx"),
            P(),
            P(),
            P(None, None, "tp"),
            P(None, None, "tp"),
            P("tp", "ctx"),
            P("tp"),
            P(None, "tp"),
        ),
        out_specs=P("ctx", "tp"),
        check_vma=False,
    )
```

time: 516 us -> 200 us (0.39); the launches traced: 508 us -> 200 us
  matrix products: 202 us -> 22 us
  local copies, waits for them, and re-layouts: 102 us -> 10.9 us
  other arithmetic: 85.9 us -> 3.35 us
  Pallas kernels: 0 us -> 45.2 us
  blocking collectives: 42.2 us -> 84.8 us
  waiting for transfers between devices: 45.5 us -> 24.5 us
  between operations: 14 us -> 0.18 us
  starting transfers between devices: 17.4 us -> 9.04 us
    dot_general x21 -> x4, matrix products: 202 us -> 22 us  [the longest x2 15.3 us: local(): lax.dot_general(piece, own_rows, (((0,), (0,)), ((), ())), preferred_elem...]
    unnamed x4 -> x1, other arithmetic: 67.5 us -> 0.01 us
    all_gather x1 -> x0, waiting for transfers between devices: 45.5 us -> none  [local(): lax.all_gather(gated, 'tp', axis=0, tiled=True)]
    pallas_call x0 -> x1, Pallas kernels: none -> 45.2 us  [long_block(): pl.pallas_call(functools.partial(block_kernel, stride=stride, unroll=unro...]
    unnamed x33 -> x28, local copies, waits for them, and re-layouts: 50.2 us -> 5.26 us
    all_gather x0 -> x1, blocking collectives: none -> 40.7 us  [local(): tokens = lax.all_gather(token_ids, 'ctx', axis=0, tiled=True)]
    ppermute x1, waiting for transfers between devices: 0.01 us -> 24.5 us  [local(): piece = lax.ppermute(mine, 'tp', route)]
    convert_element_type x5 -> x0, local copies, waits for them, and re-layouts: 18.9 us -> none  [the longest x1 9.96 us: local(): (convolved + own_skip * product.astype(jnp.float32)).astype(jnp.bfloat16)]
  transfers between devices with their start and end apart: 4 -> 2, of which waited for: 1 -> 1; matrix products, arithmetic and copies ran while one was open for 27% -> 14% of each run, Pallas kernels for 0% -> 0%
where the time goes in v1:
time: 200 us
  blocking collectives  84.8 us (42%)
  Pallas kernels  45.2 us (23%)
  waiting for transfers between devices  24.5 us (12%)
  matrix products  22 us (11%)
  local copies, waits for them, and re-layouts  10.9 us (5%)
  starting transfers between devices  9.04 us (5%)
  other arithmetic  3.35 us (2%)
    pallas_call x1, Pallas kernels, long_block(): pl.pallas_call(functools.partial(block_kernel, stride=stride, unroll=unro...  45.2 us
    all_to_all x1, blocking collectives, local(): mine = lax.all_to_all(gated, 'ctx', split_axis=0, concat_axis=0, tiled=True)  44.1 us
    all_gather x1, blocking collectives, local(): tokens = lax.all_gather(token_ids, 'ctx', axis=0, tiled=True)  40.7 us
    ppermute x1, waiting for transfers between devices, local(): piece = lax.ppermute(mine, 'tp', route)  24.5 us
    dot_general x2, matrix products, local(): lax.dot_general(piece, own_rows, (((0,), (0,)), ((), ())), preferred_elem...  15.3 us
    all_to_all x1, starting transfers between devices, local(): lax.all_to_all(long_filter.reshape(groups, chans, span), 'ctx', split_axi...  7.52 us
    unnamed x28, local copies, waits for them, and re-layouts  5.26 us
    dynamic_slice x1, local copies, waits for them, and re-layouts, local(): lax.dynamic_slice_in_dim(w_in, first, chans, 2).reshape(width, 3 * chans)  4.46 us
  transfers between devices with their start and end apart: 2, of which 1 were waited for; matrix products, arithmetic and copies ran while one was open for 14% of the time, Pallas kernels for 0%

profile of v1, /device:TPU:0, one launch (start us, length us, event | category | flops | bytes accessed | tf_op | source)
XLA Modules:
  0.0 200.0 jit_solution(15449244145049803576)
XLA Ops:
  0.0 0.0 copy-start
  0.0 7.5 %all-to-all-start = ((bf16[16,64,768]{2,1,0:T(8,128)(2,1)}), bf16[16,64,768]{2,1,0:T(8,128)(2,1)S(1)}, u32[]{:S(2)}, u32[]{:S(2)}) async-start(bf16[16,64,768]{2,1,0:T(8,128)(2,1)} %bitcast.8), calls=%async_computation | async-start | bytes 3145728 | tf_op jit(solution)/shard_map/all_to_all | solution.py:183
  7.5 0.7 reshape.30
  8.2 0.8 dynamic-slice_bitcast_fusion
  9.0 0.1 copy.21.skip_ref
  9.1 40.7 %all-gather = s32[16,1,768]{2,1,0:T(1,128)S(1)} all-gather(s32[1,1,768]{2,1,0:T(1,128)S(1)} %reshape.30), channel_id=1, replica_groups=mesh['ctx'=16,'tp'=2] {'ctx'}, dimensions={0}, use_global_device_ids=true | all-gather | bytes 52224 | tf_op jit(solution)/shard_map/all_gather | solution.py:186
  49.8 0.1 reduce
  49.9 0.0 copy-done
  49.9 0.1 constant_dynamic-slice_fusion
  50.0 0.3 reshape.33.taps_ref
  50.3 4.5 %constant_dynamic-slice_fusion.1 = bf16[4096,3,64]{2,0,1:T(8,128)(2,1)} fusion(bf16[4096,3,1024]{2,0,1:T(8,128)(2,1)} %param.17, s32[]{:T(128)S(6)} %select_n.15), kind=kLoop, calls=%fused_computation.22 | loop fusion | bytes 3145732 | tf_op jit(solution)/shard_map/dynamic_slice | solution.py:191
  54.7 0.0 copy-start.10
  54.7 4.3 %copy.22 = bf16[4096,3,64]{0,2,1:T(8,128)(2,1)} copy(bf16[4096,3,64]{2,0,1:T(8,128)(2,1)} %constant_dynamic-slice_fusion.1) | data formatting | bytes 3145728
  59.0 0.0 copy-start.8
  59.0 3.2 %fusion = f32[512]{0:T(512)S(1)} fusion(bf16[512,4096]{1,0:T(8,128)(2,1)} %param.15), kind=kLoop, calls=%fused_computation.2 | loop fusion | flops 6290944 | bytes 4196352 | tf_op jit(solution)/shard_map/reduce_sum | solution.py:189
  62.3 0.0 copy-done.10
  62.3 0.2 copy-done.8
  62.5 0.0 copy-start.2
  62.5 0.0 copy-start.3
  62.5 0.0 copy-start.4
  62.5 0.0 copy-start.5
  62.5 0.0 copy-start.6
  62.5 0.0 copy-start.7
  62.5 3.1 %fusion.15.tab_ref = bf16[192,512]{1,0:T(8,128)(2,1)S(1)} fusion(bf16[4096,192]{0,1:T(8,128)(2,1)} %bitcast.11, bf16[512,4096]{1,0:T(8,128)(2,1)S(1)} %copy-done.8, f32[4096]{0:T(1024)S(1)} %copy-done.10, f32[512]{0:T(512)S(1)} %add_rsqrt_fusion), kind=kOutput, calls=%fused_computation.16 | convolution fusion | flops 813793280 | bytes 5982208 | tf_op jit(solution)/shard_map/dot_general | solution.py:192
  65.6 0.0 copy-start.9
  65.6 0.0 all-to-all-done.h_ref
  65.6 0.0 copy-done.2
  65.6 0.0 copy-done.3
  65.6 0.0 copy-done.4
  65.7 0.0 copy-done.5
  65.7 0.0 copy-done.6
  65.7 0.0 copy-done.7
  65.7 45.2 %shard_map.136 = bf16[16,64,768]{2,1,0:T(8,128)(2,1)S(1)} custom-call(s32[48,256]{1,0:T(8,128)S(1)} %reshape.25.tok_ref, bf16[192,512]{1,0:T(8,128)(2,1)S(1)} %fusion.15.tab_ref, f32[3,192,1]{2,1,0:T(8,128)S(1)} %reshape.33.taps_ref, f32[64,1]{1,0:T(8,128)S(1)} %copy.21.skip_ref, bf16[16,64,768]{2,1,0:T(8,128)(2,1)S(1)} %all-to-all-done.h_ref, ...), custom_call_target="tpu_custom_call" | custom-call | flops 40000000000 | bytes 8000000 | tf_op jit(solution)/shard_map/pallas_call | solution.py:154
  110.8 44.1 %all_to_all.10 = bf16[16,64,768]{2,1,0:T(8,128)(2,1)S(1)} all-to-all(bf16[16,64,768]{2,1,0:T(8,128)(2,1)S(1)} %shard_map.136), channel_id=1, replica_groups=mesh['ctx'=16,'tp'=2] {'ctx'}, dimensions={0} | all-to-all | bytes 3145728 | tf_op jit(solution)/shard_map/all_to_all | solution.py:199
  155.0 1.5 collective-permute-start
  156.5 0.0 copy-done.9
  156.5 0.0 slice-start
  156.5 3.6 %fusion.11 = f32[768,2048]{1,0:T(8,128)S(1)} fusion(bf16[512,4096]{1,0:T(8,128)(2,1)} %param.15, s32[]{:T(128)S(6)} %select_n.14, s32[768]{0:T(1024)S(1)} %copy-done.9), kind=kOutput, calls=%fused_computation.13 | convolution fusion | flops 1611005952 | bytes 8391684 | tf_op jit(solution)/shard_map/dot_general | solution.py:205
  160.1 0.0 slice-start.1
  160.1 7.7 %fusion.7 = f32[768,2048]{1,0:T(8,128)} fusion(bf16[1024,768]{1,0:T(8,128)(2,1)S(1)} %bitcast.10, bf16[2048,2048]{1,0:T(8,128)(2,1)} %param.21, s32[]{:T(128)S(6)} %select_n.16), kind=kOutput, calls=%fused_computation.9 | convolution fusion | flops 3221225472 | bytes 12058628 | tf_op jit(solution)/shard_map/dot_general | solution.py:214
  167.8 24.5 %collective-permute-done = bf16[1024,768]{1,0:T(8,128)(2,1)} collective-permute-done((bf16[1024,768]{1,0:T(8,128)(2,1)S(1)}, bf16[1024,768]{1,0:T(8,128)(2,1)}, u32[]{:S(2)}, u32[]{:S(2)}) %collective-permute-start) | collective-permute-done | bytes 1572896 | tf_op jit(solution)/shard_map/ppermute | solution.py:211
  192.4 0.0 slice-done
  192.4 0.0 slice-done.1
  192.4 0.0 copy-start.1
  192.4 7.6 %add_convert_fusion = bf16[768,2048]{1,0:T(8,128)(2,1)} fusion(f32[768,2048]{1,0:T(8,128)S(1)} %fusion.11, f32[768,2048]{1,0:T(8,128)} %fusion.7, bf16[1024,768]{1,0:T(8,128)(2,1)} %collective-permute-done, bf16[2048,2048]{1,0:T(8,128)(2,1)S(1)} %bitcast.13, s32[]{:T(128)S(6)} %select_n.17), kind=kOutput, calls=%fused_computation.5 | convolution fusion | flops 3225944064 | bytes 21495812 | tf_op jit(solution)/shard_map/dot_general | solution.py:214
  200.0 0.0 copy-done.1
  (3 shorter events, 0.0 us)
Async XLA Ops:
  0.0 49.9 %copy-start = (f32[3,3,1024]{2,1,0:T(4,128)S(1)}, f32[3,3,1024]{2,1,0:T(4,128)}, u32[]{:S(2)}) copy-start(f32[3,3,1024]{2,1,0:T(4,128)} %param.18) | copy-start | bytes 110596
  0.0 65.6 %all-to-all-start = ((bf16[16,64,768]{2,1,0:T(8,128)(2,1)}), bf16[16,64,768]{2,1,0:T(8,128)(2,1)S(1)}, u32[]{:S(2)}, u32[]{:S(2)}) async-start(bf16[16,64,768]{2,1,0:T(8,128)(2,1)} %bitcast.8), calls=%async_computation | async-start | bytes 3145728 | tf_op jit(solution)/shard_map/all_to_all | solution.py:183
  54.7 7.6 %copy-start.10 = (f32[4096]{0:T(1024)S(1)}, f32[4096]{0:T(1024)}, u32[]{:S(2)}) copy-start(f32[4096]{0:T(1024)} %param.16) | copy-start | bytes 49156
  59.0 3.4 %copy-start.8 = (bf16[512,4096]{1,0:T(8,128)(2,1)S(1)}, bf16[512,4096]{1,0:T(8,128)(2,1)}, u32[]{:S(2)}) copy-start(bf16[512,4096]{1,0:T(8,128)(2,1)} %param.15) | copy-start | bytes 12582916
  62.5 3.2 %copy-start.2 = (bf16[256,256]{1,0:T(8,128)(2,1)S(1)}, bf16[256,256]{1,0:T(8,128)(2,1)}, u32[]{:S(2)}) copy-start(bf16[256,256]{1,0:T(8,128)(2,1)} %constant.51.clone.inv_ref) | copy-start | bytes 393220
  62.5 3.2 %copy-start.3 = (bf16[256,256]{1,0:T(8,128)(2,1)S(1)}, bf16[256,256]{1,0:T(8,128)(2,1)}, u32[]{:S(2)}) copy-start(bf16[256,256]{1,0:T(8,128)(2,1)} %constant.50.clone.fwd_ref) | copy-start | bytes 393220
  62.5 3.2 %copy-start.4 = (f32[112,128]{1,0:T(8,128)S(1)}, f32[112,128]{1,0:T(8,128)}, u32[]{:S(2)}) copy-start(f32[112,128]{1,0:T(8,128)} %constant.49.clone.sin_ref) | copy-start | bytes 172036
  62.5 3.2 %copy-start.5 = (f32[112,128]{1,0:T(8,128)S(1)}, f32[112,128]{1,0:T(8,128)}, u32[]{:S(2)}) copy-start(f32[112,128]{1,0:T(8,128)} %constant.48.clone.cos_ref) | copy-start | bytes 172036
  62.5 3.2 %copy-start.6 = (bf16[224,96]{1,0:T(8,128)(2,1)S(1)}, bf16[224,96]{1,0:T(8,128)(2,1)}, u32[]{:S(2)}) copy-start(bf16[224,96]{1,0:T(8,128)(2,1)} %constant.47.clone.coarse_ref) | copy-start | bytes 129028
  62.5 3.2 %copy-start.7 = (bf16[96,224]{1,0:T(8,128)(2,1)S(1)}, bf16[96,224]{1,0:T(8,128)(2,1)}, u32[]{:S(2)}) copy-start(bf16[96,224]{1,0:T(8,128)(2,1)} %constant.52.clone.back_ref) | copy-start | bytes 129028
  65.6 90.9 %copy-start.9 = (s32[768]{0:T(1024)S(1)}, s32[768]{0:T(1024)}, u32[]{:S(2)}) copy-start(s32[768]{0:T(1024)} %param.14) | copy-start | bytes 9220
  155.0 37.4 %collective-permute-start = (bf16[1024,768]{1,0:T(8,128)(2,1)S(1)}, bf16[1024,768]{1,0:T(8,128)(2,1)}, u32[]{:S(2)}, u32[]{:S(2)}) collective-permute-start(bf16[1024,768]{1,0:T(8,128)(2,1)S(1)} %bitcast.9), channel_id=1, source_target_pairs={{0,1},{1,0},{2,3},{3,2},{4,5},{5,4},{6,7},{7,6},{8,9},{9,8},{10,11... | collective-permute-start | bytes 4718600 | tf_op jit(solution)/shard_map/ppermute | solution.py:211
  156.5 35.9 %slice-start = ((s8[8388608]{0:T(1024)(128)(4,1)}), s8[4194304]{0:T(1024)(128)(4,1)S(1)}, s32[]{:S(2)}) async-start(s8[8388608]{0:T(1024)(128)(4,1)} %bitcast.12), calls=%async_computation.2 | async-start | bytes 8388608
  160.1 32.3 %slice-start.1 = ((s8[8388608]{0:T(1024)(128)(4,1)}), s8[4194304]{0:T(1024)(128)(4,1)S(1)}, s32[]{:S(2)}) async-start(s8[8388608]{0:T(1024)(128)(4,1)} %bitcast.12), calls=%async_computation.3 | async-start | bytes 8388608
  192.4 7.6 %copy-start.1 = (f32[3,3,1024]{2,1,0:T(4,128)S(1)}, f32[3,3,1024]{2,1,0:T(4,128)}, u32[]{:S(2)}) copy-start(f32[3,3,1024]{2,1,0:T(4,128)} %param.18) | copy-start | bytes 110596

commit v2 on v1

--- a/solution.py
+++ b/solution.py
@@ -48,20 +48,12 @@
     return jnp.dot(left, right, preferred_element_type=jnp.float32)
 
 
-def block_kernel(
-    tok_ref, tab_ref, taps_ref, skip_ref, h_ref,
-    coarse_ref, cos_ref, sin_ref, fwd_ref, inv_ref, back_ref,
-    out_ref, pf, hf, q_s, p_s, *, stride, unroll,
-):
+def project_kernel(tok_ref, tab_ref, taps_ref, q_ref, p_ref):
     half = jnp.bfloat16
     full = jnp.float32
-    sources, chans, span = h_ref.shape
-    per = span // lanes
-    blocks = sources * per
+    blocks, chans, _ = q_ref.shape
     vocab = tab_ref.shape[1]
     rows3 = 3 * chans
-    padded = cos_ref.shape[0]
-
     words = lax.broadcasted_iota(jnp.int32, (vocab, wide), 0)
     lane = lax.broadcasted_iota(jnp.int32, (rows3, lanes), 1)
 
@@ -81,20 +73,50 @@
             one_back, two_back = once, twice
             key = short[chans : 2 * chans].astype(full)
             value = short[2 * chans :].astype(full)
-            product = (key * value).astype(half)
             at = step * (wide // lanes) + part
-            q_s[at] = short[:chans]
-            p_s[at] = product
-            pf[pl.ds(at, chans, stride=stride), :] = product.astype(full)
+            q_ref[at] = short[:chans]
+            p_ref[at] = (key * value).astype(half)
         return one_back, two_back
 
     zero = jnp.zeros((rows3, lanes), full)
     lax.fori_loop(0, blocks * lanes // wide, project, (zero, zero))
+
+
+def conv_kernel(
+    q_ref, p_ref, h_ref, skip_ref,
+    coarse_ref, cos_ref, sin_ref, fwd_ref, inv_ref, back_ref,
+    got_ref, pf, hf, ready, send_x, recv_x, send_y, recv_y, keep,
+    *, stride, unroll, chunks, groups, parts,
+):
+    half = jnp.bfloat16
+    full = jnp.float32
+    sources, chans, span = h_ref.shape
+    per = span // lanes
+    blocks = sources * per
+    padded = cos_ref.shape[0]
+    some = chans // chunks
+    me = lax.axis_index("ctx")
+    row = lax.axis_index("tp")
+    mesh_ids = pl.DeviceIdType.MESH
+
+    barrier = pltpu.get_barrier_semaphore()
+
+    def greet(step, _):
+        peer = lax.rem(me + step, groups)
+        pl.semaphore_signal(barrier, inc=1, device_id=(peer, row), device_id_type=mesh_ids)
+        return 0
+
+    lax.fori_loop(1, groups, greet, 0)
+    for step in range(1, parts):
+        peer = lax.rem(row + step, parts)
+        pl.semaphore_signal(barrier, inc=1, device_id=(me, peer), device_id_type=mesh_ids)
 
     def take(source, _):
         for part in range(per):
             tile = h_ref[source, :, part * lanes : (part + 1) * lanes]
-            hf[pl.ds(source * per + part, chans, stride=stride), :] = tile.astype(full)
+            at = source * per + part
+            hf[pl.ds(at, chans, stride=stride), :] = tile.astype(full)
+            pf[pl.ds(at, chans, stride=stride), :] = p_ref[at].astype(full)
         return 0
 
     lax.fori_loop(0, sources, take, 0)
@@ -129,44 +151,156 @@
             pf[here, :] = mul(back_ref[...], stacked)
         return 0
 
-    lax.fori_loop(0, chans // unroll, convolve, 0)
-
-    def finish(source, _):
-        for part in range(per):
-            at = source * per + part
-            convolved = pf[pl.ds(at, chans, stride=stride), :]
-            skipped = (convolved + skip_ref[...] * p_s[at].astype(full)).astype(half)
-            gated = q_s[at].astype(full) * skipped.astype(full)
-            out_ref[source, :, part * lanes : (part + 1) * lanes] = gated.astype(half)
-        return 0
-
-    lax.fori_loop(0, sources, finish, 0)
-
-
-def long_block(tokens, table, taps, skip, filters, chans):
-    groups, _, span = filters.shape
+    def across(chunk, step):
+        peer = lax.rem(me + step, groups)
+        return pltpu.make_async_remote_copy(
+            src_ref=ready.at[chunk, peer],
+            dst_ref=got_ref.at[row, me, chunk],
+            send_sem=send_x.at[chunk, step],
+            recv_sem=recv_x.at[chunk, step],
+            device_id=(peer, row),
+            device_id_type=mesh_ids,
+        )
+
+    def arrival(chunk, step):
+        origin = lax.rem(me - step + groups, groups)
+        slot = got_ref.at[row, origin, chunk]
+        return pltpu.make_async_remote_copy(
+            src_ref=slot,
+            dst_ref=slot,
+            send_sem=send_x.at[chunk, step],
+            recv_sem=recv_x.at[chunk, step],
+            device_id=(lax.rem(me + step, groups), row),
+            device_id_type=mesh_ids,
+        )
+
+    def onward(chunk, step, hop, source, slot):
+        return pltpu.make_async_remote_copy(
+            src_ref=source,
+            dst_ref=slot,
+            send_sem=send_y.at[hop, chunk, step],
+            recv_sem=recv_y.at[hop, chunk, step],
+            device_id=(me, lax.rem(row + hop, parts)),
+            device_id_type=mesh_ids,
+        )
+
+    def forward(chunk):
+        def relay(step, _):
+            arrival(chunk, step).wait_recv()
+            slot = got_ref.at[row, lax.rem(me - step + groups, groups), chunk]
+            for hop in range(1, parts):
+                onward(chunk, step, hop, slot, slot).start()
+            return 0
+
+        lax.fori_loop(1, groups, relay, 0)
+
+    for chunk in range(chunks):
+        low = chunk * some
+        lax.fori_loop(low // unroll, (low + some) // unroll, convolve, 0)
+
+        def finish(source, _):
+            for part in range(per):
+                at = source * per + part
+                convolved = pf[pl.ds(low * stride + at, some, stride=stride), :]
+                product = p_ref[at, low : low + some, :].astype(full)
+                skipped = (convolved + skip_ref[low : low + some, :] * product).astype(half)
+                gated = q_ref[at, low : low + some, :].astype(full) * skipped.astype(full)
+                ready[chunk, source, :, part * lanes : (part + 1) * lanes] = gated.astype(half)
+            return 0
+
+        lax.fori_loop(0, sources, finish, 0)
+        if chunk == 0:
+            pl.semaphore_wait(barrier, groups - 1 + parts - 1)
+
+        def launch(step, _):
+            across(chunk, step).start()
+            return 0
+
+        lax.fori_loop(1, groups, launch, 0)
+        own = got_ref.at[row, me, chunk]
+        pltpu.make_async_copy(ready.at[chunk, me], own, keep.at[chunk]).start()
+        for hop in range(1, parts):
+            onward(chunk, 0, hop, ready.at[chunk, me], own).start()
+        if chunk > 0:
+            forward(chunk - 1)
+    forward(chunks - 1)
+
+    for chunk in range(chunks):
+        own = got_ref.at[row, me, chunk]
+        pltpu.make_async_copy(ready.at[chunk, me], own, keep.at[chunk]).wait()
+
+        def settle(step, _):
+            across(chunk, step).wait_send()
+            return 0
+
+        lax.fori_loop(1, groups, settle, 0)
+
+        def settle_y(step, _):
+            origin = lax.rem(me - step + groups, groups)
+            for hop in range(1, parts):
+                mine = got_ref.at[row, origin, chunk]
+                theirs = got_ref.at[lax.rem(row - hop + parts, parts), origin, chunk]
+                onward(chunk, step, hop, mine, mine).wait_send()
+                onward(chunk, step, hop, theirs, theirs).wait_recv()
+            return 0
+
+        lax.fori_loop(0, groups, settle_y, 0)
+
+
+def project_all(tokens, table, taps, chans):
+    length = tokens.shape[0]
+    vmem = pl.BlockSpec(memory_space=pltpu.VMEM)
+    shape = jax.ShapeDtypeStruct((length // lanes, chans, lanes), jnp.bfloat16)
+    return pl.pallas_call(
+        project_kernel,
+        out_shape=(shape, shape),
+        in_specs=[vmem] * 3,
+        out_specs=(vmem, vmem),
+        compiler_params=pltpu.CompilerParams(vmem_limit_bytes=24 * 1024 * 1024),
+        cost_estimate=pl.CostEstimate(
+            flops=2 * table.shape[0] * table.shape[1] * length * 4,
+            bytes_accessed=8_000_000,
+            transcendentals=0,
+        ),
+    )(tokens.reshape(length // wide, wide), table, taps)
+
+
+def long_block(query, product, filters, skip, groups, parts):
+    _, chans, span = filters.shape
     length = groups * span
     blocks = length // lanes
     stride = blocks + 8
     tables = transform_tables(length)
-    unroll = math.gcd(chans, 4)
+    chunks = 2 if chans % 32 == 0 else 1
+    some = chans // chunks
+    unroll = math.gcd(some, 4)
     vmem = pl.BlockSpec(memory_space=pltpu.VMEM)
+    dma = pltpu.SemaphoreType.DMA
     return pl.pallas_call(
-        functools.partial(block_kernel, stride=stride, unroll=unroll),
-        out_shape=jax.ShapeDtypeStruct((groups, chans, span), jnp.bfloat16),
-        in_specs=[vmem] * 11,
-        out_specs=vmem,
+        functools.partial(
+            conv_kernel,
+            stride=stride, unroll=unroll, chunks=chunks, groups=groups, parts=parts,
+        ),
+        out_shape=jax.ShapeDtypeStruct((parts, groups, chunks, some, span), jnp.bfloat16),
+        in_specs=[vmem] * 10,
+        out_specs=pl.BlockSpec(memory_space=pl.ANY),
         scratch_shapes=[
             pltpu.VMEM((chans * stride, lanes), jnp.float32),
             pltpu.VMEM((chans * stride, lanes), jnp.float32),
-            pltpu.VMEM((blocks, chans, lanes), jnp.bfloat16),
-            pltpu.VMEM((blocks, chans, lanes), jnp.bfloat16),
+            pltpu.VMEM((chunks, groups, some, span), jnp.bfloat16),
+            dma((chunks, groups)),
+            dma((chunks, groups)),
+            dma((parts, chunks, groups)),
+            dma((parts, chunks, groups)),
+            dma((chunks,)),
         ],
-        compiler_params=pltpu.CompilerParams(vmem_limit_bytes=48 * 1024 * 1024),
+        compiler_params=pltpu.CompilerParams(
+            vmem_limit_bytes=48 * 1024 * 1024, collective_id=0, has_side_effects=True
+        ),
         cost_estimate=pl.CostEstimate(
             flops=40_000_000_000, bytes_accessed=8_000_000, transcendentals=0
         ),
-    )(tokens.reshape(length // wide, wide), table, taps, skip, filters, *map(jnp.asarray, tables))
+    )(query, product, filters, skip, *map(jnp.asarray, tables))
 
 
 def local(token_ids, embed_table, norm_gain, w_in, short_taps, long_filter, skip_gain, w_out):
@@ -180,10 +314,11 @@
     first = lax.axis_index("ctx") * chans
     span = token_ids.shape[0]
 
+    tokens = lax.all_gather(token_ids, "ctx", axis=0, tiled=True)
+    tokens, waiting = lax.optimization_barrier((tokens, long_filter))
     filters = lax.all_to_all(
-        long_filter.reshape(groups, chans, span), "ctx", split_axis=0, concat_axis=0, tiled=True
+        waiting.reshape(groups, chans, span), "ctx", split_axis=0, concat_axis=0, tiled=True
     )
-    tokens = lax.all_gather(token_ids, "ctx", axis=0, tiled=True)
 
     rows = embed_table.astype(jnp.float32)
     scale = lax.rsqrt(jnp.mean(rows * rows, axis=1, keepdims=True) + norm_eps)
@@ -195,26 +330,18 @@
     taps = lax.dynamic_slice_in_dim(short_taps, first, chans, 2).reshape(-1, 3 * chans, 1)
     skip = lax.dynamic_slice_in_dim(skip_gain, first, chans)[:, None]
 
-    gated = long_block(tokens, table, taps, skip, filters, chans)
-    mine = lax.all_to_all(gated, "ctx", split_axis=0, concat_axis=0, tiled=True)
-    mine = mine.reshape(local_channels, span)
+    query, product = project_all(tokens, table, taps, chans)
+    gated = long_block(query, product, filters, skip, groups, parts)
+    gated = gated.reshape(parts * local_channels, span)
 
     columns = w_out.shape[1]
     one_hot = (token_ids[:, None] == jnp.arange(vocab, dtype=jnp.int32)[None, :]).astype(half)
     own_embed = lax.dynamic_slice_in_dim(embed_table, me * columns, columns, 1)
-    total = jnp.dot(one_hot, own_embed, preferred_element_type=jnp.float32)
-    for step in range(parts):
-        if step == 0:
-            piece = mine
-        else:
-            route = [(i, (i + step) % parts) for i in range(parts)]
-            piece = lax.ppermute(mine, "tp", route)
-        owner = lax.rem(me - step + parts, parts)
-        own_rows = lax.dynamic_slice_in_dim(w_out, owner * local_channels, local_channels, 0)
-        total = total + lax.dot_general(
-            piece, own_rows, (((0,), (0,)), ((), ())), preferred_element_type=jnp.float32
-        )
-    return total.astype(half)
+    residual = jnp.dot(one_hot, own_embed, preferred_element_type=jnp.float32)
+    total = lax.dot_general(
+        gated, w_out, (((0,), (0,)), ((), ())), preferred_element_type=jnp.float32
+    )
+    return (residual + total).astype(half)
 
 
 def solution(mesh):

time: 200 us -> 149 us (0.74)
  blocking collectives: 84.8 us -> 23.2 us
  Pallas kernels: 45.2 us -> 85 us
  waiting for transfers between devices: 24.5 us -> 0.01 us
  starting transfers between devices: 9.04 us -> 3.71 us
  local copies, waits for them, and re-layouts: 10.9 us -> 16.1 us
  matrix products: 22 us -> 16.9 us
    all_to_all x1 -> x0, blocking collectives: 44.1 us -> none  [local(): mine = lax.all_to_all(gated, 'ctx', split_axis=0, concat_axis=0, tiled=True)]
    pallas_call x1 -> x2, Pallas kernels: 45.2 us -> 85 us  [the longest x1 69 us: long_block(): pl.pallas_call(functools.partial(conv_kernel, stride=stride, unroll=unrol...]
    ppermute x1 -> x0, waiting for transfers between devices: 24.5 us -> none  [local(): piece = lax.ppermute(mine, 'tp', route)]
    all_gather x1, blocking collectives: 40.7 us -> 23.2 us  [local(): tokens = lax.all_gather(token_ids, 'ctx', axis=0, tiled=True)]
    unnamed x28 -> x32, local copies, waits for them, and re-layouts: 5.26 us -> 10.4 us
    dot_general x3 -> x2, matrix products: 18.9 us -> 13.9 us  [the longest x1 10.3 us: local(): lax.dot_general(gated, w_out, (((0,), (0,)), ((), ())), preferred_element...]
    all_to_all x1, starting transfers between devices: 7.52 us -> 3.71 us  [local(): lax.all_to_all(waiting.reshape(groups, chans, span), 'ctx', split_axis=0,...]
  transfers between devices with their start and end apart: 2 -> 1, of which waited for: 1 -> 0; matrix products, arithmetic and copies ran while one was open for 14% -> 11% of each run, Pallas kernels for 0% -> 11%
where the time goes in v2:
time: 149 us; the launch traced here: 148 us
  Pallas kernels  85 us (57%)
  blocking collectives  23.2 us (16%)
  matrix products  16.9 us (11%)
  local copies, waits for them, and re-layouts  16.1 us (11%)
  starting transfers between devices  3.71 us (2%)
  other arithmetic  3.24 us (2%)
    pallas_call x1, Pallas kernels, long_block(): pl.pallas_call(functools.partial(conv_kernel, stride=stride, unroll=unrol...  69 us
    all_gather x1, blocking collectives, local(): tokens = lax.all_gather(token_ids, 'ctx', axis=0, tiled=True)  23.2 us
    pallas_call x1, Pallas kernels, project_all(): pl.pallas_call(project_kernel, out_shape=(shape, shape), in_specs=[vmem]...  16 us
    unnamed x32, local copies, waits for them, and re-layouts  10.4 us
    dot_general x1, matrix products, local(): lax.dot_general(gated, w_out, (((0,), (0,)), ((), ())), preferred_element...  10.3 us
    dynamic_slice x1, local copies, waits for them, and re-layouts, local(): lax.dynamic_slice_in_dim(w_in, first, chans, 2).reshape(width, 3 * chans)  4.46 us
    all_to_all x1, starting transfers between devices, local(): lax.all_to_all(waiting.reshape(groups, chans, span), 'ctx', split_axis=0,...  3.71 us
    dot_general x1, matrix products, local(): residual = jnp.dot(one_hot, own_embed, preferred_element_type=jnp.float32)  3.59 us
  transfers between devices with their start and end apart: 1, of which 0 were waited for; matrix products, arithmetic and copies ran while one was open for 11% of the time, Pallas kernels for 11%

profile of v2, /device:TPU:0, one launch (start us, length us, event | category | flops | bytes accessed | tf_op | source)
XLA Modules:
  0.0 148.3 jit_solution(11655717708928865659)
XLA Ops:
  0.0 0.0 copy-start
  0.0 0.7 reshape.30
  0.7 23.2 %all-gather = s32[16,1,768]{2,1,0:T(1,128)S(1)} all-gather(s32[1,1,768]{2,1,0:T(1,128)S(1)} %reshape.30), channel_id=1, replica_groups=mesh['ctx'=16,'tp'=2] {'ctx'}, dimensions={0}, use_global_device_ids=true | all-gather | bytes 52224 | tf_op jit(solution)/shard_map/all_gather | solution.py:317
  23.9 3.7 %all-to-all-start = ((bf16[16,64,768]{2,1,0:T(8,128)(2,1)}), bf16[16,64,768]{2,1,0:T(8,128)(2,1)S(1)}, u32[]{:S(2)}, u32[]{:S(2)}) async-start(bf16[16,64,768]{2,1,0:T(8,128)(2,1)} %bitcast.9), calls=%async_computation | async-start | bytes 3145728 | tf_op jit(solution)/shard_map/all_to_all | solution.py:319
  27.6 0.8 dynamic-slice_bitcast_fusion
  28.4 0.1 copy.21.skip_ref
  28.5 0.0 copy-done
  28.5 0.1 constant_dynamic-slice_fusion
  28.6 0.3 reshape.32.taps_ref
  28.9 4.5 %constant_dynamic-slice_fusion.1 = bf16[4096,3,64]{2,0,1:T(8,128)(2,1)} fusion(bf16[4096,3,1024]{2,0,1:T(8,128)(2,1)} %param.17, s32[]{:T(128)S(6)} %select_n.9), kind=kLoop, calls=%fused_computation.15 | loop fusion | bytes 3145732 | tf_op jit(solution)/shard_map/dynamic_slice | solution.py:326
  33.3 0.0 copy-start.14
  33.3 4.3 %copy.22 = bf16[4096,3,64]{0,2,1:T(8,128)(2,1)} copy(bf16[4096,3,64]{2,0,1:T(8,128)(2,1)} %constant_dynamic-slice_fusion.1) | data formatting | bytes 3145728
  37.6 0.0 copy-start.11
  37.6 3.2 %fusion = f32[512]{0:T(512)S(1)} fusion(bf16[512,4096]{1,0:T(8,128)(2,1)} %param.15), kind=kLoop, calls=%fused_computation.2 | loop fusion | flops 6290944 | bytes 4196352 | tf_op jit(solution)/shard_map/reduce_sum | solution.py:324
  40.9 0.0 copy-done.14
  40.9 0.2 copy-done.11
  41.1 3.0 %fusion.8.tab_ref = bf16[192,512]{1,0:T(8,128)(2,1)S(1)} fusion(bf16[4096,192]{0,1:T(8,128)(2,1)} %bitcast.10, bf16[512,4096]{1,0:T(8,128)(2,1)S(1)} %copy-done.11, f32[4096]{0:T(1024)S(1)} %copy-done.14, f32[512]{0:T(512)S(1)} %add_rsqrt_fusion), kind=kOutput, calls=%fused_computation.11 | convolution fusion | flops 813793280 | bytes 5982208 | tf_op jit(solution)/shard_map/dot_general | solution.py:327
  44.1 0.0 copy-start.1
  44.1 0.0 copy-start.2
  44.1 0.0 copy-start.3
  44.2 0.0 copy-start.4
  44.2 0.0 copy-start.5
  44.2 0.0 copy-start.6
  44.2 16.0 %shard_map.136 = (bf16[96,64,128]{2,1,0:T(8,128)(2,1)S(1)}, bf16[96,64,128]{2,1,0:T(8,128)(2,1)S(1)}) custom-call(s32[48,256]{1,0:T(8,128)S(1)} %reshape.25.tok_ref, bf16[192,512]{1,0:T(8,128)(2,1)S(1)} %fusion.8.tab_ref, f32[3,192,1]{2,1,0:T(8,128)S(1)} %reshape.32.taps_ref), custom_call_target="tpu_custom_call" | custom-call | flops 9663676416 | bytes 8000000 | tf_op jit(solution)/shard_map/pallas_call | solution.py:254
  60.2 0.0 copy-start.7
  60.2 1.1 copy-done.7
  61.3 0.0 copy-start.9
  61.3 1.2 copy-done.9
  62.5 0.0 all-to-all-done.h_ref
  62.5 0.0 copy-done.1
  62.5 0.0 copy-done.2
  62.5 0.0 copy-done.3
  62.5 0.0 copy-done.4
  62.5 0.0 copy-done.5
  62.5 0.0 copy-done.6
  62.5 0.0 copy-start.8
  62.6 1.4 copy-done.8
  64.0 0.0 copy-start.10
  64.0 1.4 copy-done.10
  65.4 69.0 %shard_map.137 = bf16[2,16,2,32,768]{4,3,2,1,0:T(8,128)(2,1)} custom-call(bf16[96,64,128]{2,1,0:T(8,128)(2,1)S(1)} %copy-done.8, bf16[96,64,128]{2,1,0:T(8,128)(2,1)S(1)} %copy-done.10, bf16[16,64,768]{2,1,0:T(8,128)(2,1)S(1)} %all-to-all-done.h_ref, f32[64,1]{1,0:T(8,128)S(1)} %copy.21.skip_ref, bf16[224,96]{1,0:T(8,128)(2,1)S(1)} %copy-done.5, ...), custom_call_target="tpu_custom_call" | custom-call | flops 40000000000 | bytes 8000000 | tf_op jit(solution)/shard_map/pallas_call | solution.py:279
  134.4 0.0 copy-start.12
  134.4 0.0 copy-start.13
  134.4 10.3 %fusion.13 = f32[768,2048]{1,0:T(8,128)S(1)} fusion(bf16[2048,768]{1,0:T(8,128)(2,1)} %bitcast.12, bf16[2048,2048]{1,0:T(8,128)(2,1)} %param.21), kind=kOutput, calls=%fused_computation.18 | convolution fusion | flops 6442450944 | bytes 17825792 | tf_op jit(solution)/shard_map/dot_general | solution.py:341
  144.7 0.0 copy-done.12
  144.7 0.0 copy-done.13
  144.7 3.6 %add_convert_fusion = bf16[768,2048]{1,0:T(8,128)(2,1)} fusion(f32[768,2048]{1,0:T(8,128)S(1)} %fusion.13, bf16[512,4096]{1,0:T(8,128)(2,1)S(1)} %copy-done.12, s32[]{:T(128)S(6)} %select_n.8, s32[768]{0:T(1024)S(1)} %copy-done.13), kind=kOutput, calls=%fused_computation.5 | convolution fusion | flops 1614151680 | bytes 11538436 | tf_op jit(solution)/shard_map/dot_general | solution.py:340
  (2 shorter events, 0.0 us)
Async XLA Ops:
  0.0 28.5 %copy-start = (f32[3,3,1024]{2,1,0:T(4,128)S(1)}, f32[3,3,1024]{2,1,0:T(4,128)}, u32[]{:S(2)}) copy-start(f32[3,3,1024]{2,1,0:T(4,128)} %param.18) | copy-start | bytes 110596
  23.9 38.6 %all-to-all-start = ((bf16[16,64,768]{2,1,0:T(8,128)(2,1)}), bf16[16,64,768]{2,1,0:T(8,128)(2,1)S(1)}, u32[]{:S(2)}, u32[]{:S(2)}) async-start(bf16[16,64,768]{2,1,0:T(8,128)(2,1)} %bitcast.9), calls=%async_computation | async-start | bytes 3145728 | tf_op jit(solution)/shard_map/all_to_all | solution.py:319
  33.3 7.6 %copy-start.14 = (f32[4096]{0:T(1024)S(1)}, f32[4096]{0:T(1024)}, u32[]{:S(2)}) copy-start(f32[4096]{0:T(1024)} %param.16) | copy-start | bytes 49156
  37.6 3.4 %copy-start.11 = (bf16[512,4096]{1,0:T(8,128)(2,1)S(1)}, bf16[512,4096]{1,0:T(8,128)(2,1)}, u32[]{:S(2)}) copy-start(bf16[512,4096]{1,0:T(8,128)(2,1)} %param.15) | copy-start | bytes 12582916
  44.1 18.4 %copy-start.1 = (bf16[256,256]{1,0:T(8,128)(2,1)S(1)}, bf16[256,256]{1,0:T(8,128)(2,1)}, u32[]{:S(2)}) copy-start(bf16[256,256]{1,0:T(8,128)(2,1)} %constant.41.clone.inv_ref) | copy-start | bytes 393220
  44.1 18.4 %copy-start.2 = (bf16[256,256]{1,0:T(8,128)(2,1)S(1)}, bf16[256,256]{1,0:T(8,128)(2,1)}, u32[]{:S(2)}) copy-start(bf16[256,256]{1,0:T(8,128)(2,1)} %constant.40.clone.fwd_ref) | copy-start | bytes 393220
  44.1 18.4 %copy-start.3 = (f32[112,128]{1,0:T(8,128)S(1)}, f32[112,128]{1,0:T(8,128)}, u32[]{:S(2)}) copy-start(f32[112,128]{1,0:T(8,128)} %constant.39.clone.sin_ref) | copy-start | bytes 172036
  44.2 18.4 %copy-start.4 = (f32[112,128]{1,0:T(8,128)S(1)}, f32[112,128]{1,0:T(8,128)}, u32[]{:S(2)}) copy-start(f32[112,128]{1,0:T(8,128)} %constant.38.clone.cos_ref) | copy-start | bytes 172036
  44.2 18.3 %copy-start.5 = (bf16[224,96]{1,0:T(8,128)(2,1)S(1)}, bf16[224,96]{1,0:T(8,128)(2,1)}, u32[]{:S(2)}) copy-start(bf16[224,96]{1,0:T(8,128)(2,1)} %constant.37.clone.coarse_ref) | copy-start | bytes 129028
  44.2 18.3 %copy-start.6 = (bf16[96,224]{1,0:T(8,128)(2,1)S(1)}, bf16[96,224]{1,0:T(8,128)(2,1)}, u32[]{:S(2)}) copy-start(bf16[96,224]{1,0:T(8,128)(2,1)} %constant.42.clone.back_ref) | copy-start | bytes 129028
  60.2 1.1 copy-start.7
  61.3 1.2 copy-start.9
  62.5 1.4 copy-start.8
  64.0 1.4 copy-start.10
  134.4 10.3 %copy-start.12 = (bf16[512,4096]{1,0:T(8,128)(2,1)S(1)}, bf16[512,4096]{1,0:T(8,128)(2,1)}, u32[]{:S(2)}) copy-start(bf16[512,4096]{1,0:T(8,128)(2,1)} %param.15) | copy-start | bytes 12582916
  134.4 10.3 %copy-start.13 = (s32[768]{0:T(1024)S(1)}, s32[768]{0:T(1024)}, u32[]{:S(2)}) copy-start(s32[768]{0:T(1024)} %param.14) | copy-start | bytes 9220
